TPU v7x, 32 devices: a whole 2x2x4 slice. The times are simulated.
32 devices in a mesh: dp: 2 (over x), tensor: 4 (over y, core), grid: 4 (over z).
Axes of the slice: x: 2, y: 2, z: 4, core: 2. Of those that a mesh axis runs over, the one named last changes fastest.
Arguments:
- tokens: bfloat16 [1536, 8192], P('dp', 'grid'), may hold values from -6 to 6
- cotangents: bfloat16 [2, 1536, 1024], P(None, 'dp', 'tensor'), may hold values from -0.03125 to 0.03125
- left_stat: float32 [2, 8192, 8192], P(None, ('dp', 'tensor'), 'grid'), may hold values from -6 to 6
- right_stat: float32 [2, 1024, 1024], P(None, ('dp', 'tensor'), 'grid'), may hold values from -6 to 6
- left_root: bfloat16 [2, 8192, 8192], P(None, ('dp', 'tensor'), 'grid'), may hold values from -0.3125 to 0.3125
- right_root: bfloat16 [2, 1024, 1024], P(None, 'grid'), as said below
- momentum: float32 [2, 8192, 1024], P(None, ('dp', 'tensor', 'grid')), may hold values from -6 to 6
Outputs:
- new_left: float32 [2, 8192, 8192], P(None, ('dp', 'tensor'), 'grid')
- new_right: float32 [2, 1024, 1024], P(None, ('dp', 'tensor'), 'grid')
- new_momentum: float32 [2, 8192, 1024], P(None, ('dp', 'tensor', 'grid'))
Inputs may be any that keep to these rules, and one draw needn't show every extreme that they name: `right_root`: each of the two factors is exactly symmetric.
All inputs are finite; a program needn't handle non-finite values.
Results may differ from a plain program's by a relative error of at most 0.0023.
Values may be sent and summed in bfloat16 or wider, within the bound.
No kernel may reach another device: no remote copies, remote signals or barrier semaphores. Data moves between devices by JAX's collectives and lax.ppermute only.
A program may use at most 128 MiB of HBM per device.

v0:
```python
import jax
import jax.numpy as jnp
from jax import lax
from jax.sharding import PartitionSpec as P

stat_decay = 0.9
momentum_decay = 0.9


def spread(shard, axis, root):
    mine = lax.axis_index(axis) == root
    return lax.psum(jnp.where(mine, shard, jnp.zeros_like(shard)), axis)


def shards(tokens, cotangents, left_stat, right_stat, left_root, right_root, momentum):
    partial_grad = jnp.einsum("tr,pto->pro", tokens, cotangents, preferred_element_type=jnp.float32)
    summed = lax.psum(partial_grad, "dp")
    grad_rows = lax.all_gather(summed.astype(jnp.bfloat16), "tensor", axis=2, tiled=True)
    block_rows = left_stat.shape[1]
    grid_rows = left_stat.shape[2]
    learner = lax.axis_index("dp") * lax.axis_size("tensor") + lax.axis_index("tensor")
    first_row = learner * block_rows
    source = first_row // grid_rows
    offset = first_row % grid_rows
    selected = lax.dynamic_slice_in_dim(grad_rows, offset, block_rows, 1)
    own_rows = spread(selected, "grid", source)
    gram_left = jnp.einsum("pak,pbk->pab", own_rows, grad_rows, preferred_element_type=jnp.float32)
    new_left = stat_decay * left_stat + (1.0 - stat_decay) * gram_left
    column_width = right_stat.shape[2]
    column_block = lax.dynamic_slice_in_dim(
        own_rows, lax.axis_index("grid") * column_width, column_width, 2
    )
    right_term = jnp.einsum(
        "pak,pac->pkc", own_rows, column_block, preferred_element_type=jnp.float32
    )
    gram_right = lax.psum_scatter(right_term, ("dp", "tensor"), scatter_dimension=1, tiled=True)
    new_right = stat_decay * right_stat + (1.0 - stat_decay) * gram_right
    applied = lax.psum_scatter(
        jnp.einsum("pab,pbk->apk", left_root, grad_rows, preferred_element_type=jnp.float32),
        "grid",
        scatter_dimension=0,
        tiled=True,
    )
    widened_rows = lax.all_gather(right_root, "grid", axis=1, tiled=True).astype(jnp.float32)
    update = jnp.einsum(
        "mpk,pkc->mpc",
        applied,
        widened_rows,
        precision=lax.Precision.HIGHEST,
        preferred_element_type=jnp.float32,
    )
    new_momentum = momentum_decay * momentum + jnp.transpose(update, (1, 0, 2))
    return (new_left, new_right, new_momentum)


def solution(mesh):
    return jax.shard_map(
        shards,
        mesh=mesh,
        in_specs=(
            P("dp", "grid"),
            P(None, "dp", "tensor"),
            P(None, ("dp", "tensor"), "grid"),
            P(None, ("dp", "tensor"), "grid"),
            P(None, ("dp", "tensor"), "grid"),
            P(None, "grid", None),
            P(None, ("dp", "tensor", "grid"), None),
        ),
        out_specs=(
            P(None, ("dp", "tensor"), "grid"),
            P(None, ("dp", "tensor"), "grid"),
            P(None, ("dp", "tensor", "grid"), None),
        ),
        check_vma=False,
    )
```

profile of v0, /device:TPU:0, one launch (start us, length us, event | category | flops | bytes accessed | tf_op | source)
XLA Modules:
  0.0 623.4 jit_solution(15898698768469071698)
XLA Ops:
  7.2 0.0 copy-start
  7.2 0.0 all-gather.3.cloned.1.call-start
  7.2 1.8 copy-done
  9.1 5.0 convolution_bitcast_fusion
  14.0 102.3 %all-reduce.4 = bf16[2,2048,256]{1,2,0:T(8,128)(2,1)} all-reduce(f32[2,2048,256]{1,2,0:T(8,128)} %convolution_bitcast_fusion), channel_id=1, replica_groups=mesh['dp'=2,'tensor'=4,'grid'=4] {'dp'}, use_global_device_ids=true, to_apply=%region_0.0 | all-reduce | flops 1048576 | bytes 6291456 | tf_op jit(solution)/shard_map/psum | solution.py:17
  116.3 0.0 all-gather.3.cloned.1.call-update
  116.3 0.0 all-reduce.3.cloned.1.call-start
  116.4 58.7 %all-gather.3.cloned.1.call-done = bf16[2,2048,1024]{1,2,0:T(8,128)(2,1)} async-done(((bf16[2,2048,256]{1,2,0:T(8,128)(2,1)}), bf16[2,2048,1024]{1,2,0:T(8,128)(2,1)}) %all-gather.3.cloned.1.call-update) | async-done | bytes 8388624 | tf_op jit(solution)/shard_map/all_gather | solution.py:18
  175.1 5.5 dynamic-slice_select_fusion
  180.5 0.0 all-reduce.3.cloned.1.call-update
  180.6 0.0 reduce-scatter.3.cloned.1.call-start
  180.6 155.1 %all-reduce.3.cloned.1.call-done = bf16[2,1024,1024]{1,2,0:T(8,128)(2,1)} async-done(((bf16[2,1024,1024]{1,2,0:T(8,128)(2,1)}), bf16[2,1024,1024]{1,2,0:T(8,128)(2,1)}) %all-reduce.3.cloned.1.call-update) | async-done | bytes 4194320 | tf_op jit(solution)/shard_map/psum | solution.py:12
  335.7 5.1 fusion.1
  340.8 0.0 reduce-scatter.3.cloned.1.call-update
  340.8 0.0 all-gather.5.cloned.1.call-start
  340.9 0.5 all-gather.5.cloned.1.call-update
  341.4 0.2 reduce-scatter.5.cloned.1.call-start
  341.6 15.9 %convolution_bitcast_fusion.1 = f32[1024,2,1024]{2,0,1:T(8,128)} fusion(bf16[2,2048,1024]{1,2,0:T(8,128)(2,1)} %all-gather.3.cloned.1.call-done, bf16[2,1024,2048]{2,1,0:T(8,128)(2,1)} %param.11), kind=kOutput, calls=%fused_computation.3 | convolution fusion | flops 8589934592 | bytes 25165824 | tf_op jit(solution)/shard_map/pab,pbk->apk/dot_general | solution.py:39
  357.5 0.0 reduce-scatter.5.cloned.1.call-update
  357.6 0.0 copy-start.2
  357.6 20.4 %multiply_add_fusion = f32[2,1024,2048]{2,1,0:T(8,128)} fusion(f32[2,1024,2048]{2,1,0:T(8,128)} %param.9, bf16[2,1024,1024]{1,2,0:T(8,128)(2,1)} %all-reduce.3.cloned.1.call-done, bf16[2,2048,1024]{1,2,0:T(8,128)(2,1)} %all-gather.3.cloned.1.call-done), kind=kOutput, calls=%fused_computation | convolution fusion | flops 8602517504 | bytes 46137344 | tf_op jit(solution)/shard_map/pak,pbk->pab/dot_general | solution.py:27
  378.0 3.0 reduce-scatter.3.cloned.1.call-done
  381.1 0.0 copy-done.2
  381.1 0.0 copy-start.1
  381.1 1.8 multiply_add_fusion.2
  382.9 80.3 %all-gather.5.cloned.1.call-done = bf16[2,1024,1024]{2,1,0:T(8,128)(2,1)} async-done(((bf16[2,256,1024]{2,1,0:T(8,128)(2,1)}), bf16[2,1024,1024]{2,1,0:T(8,128)(2,1)}) %all-gather.5.cloned.1.call-update) | async-done | bytes 4194320 | tf_op jit(solution)/shard_map/all_gather | solution.py:44
  463.2 145.3 %reduce-scatter.5.cloned.1.call-done = f32[256,2,1024]{2,0,1:T(8,128)} async-done(((f32[1024,2,1024]{2,0,1:T(8,128)}), f32[256,2,1024]{2,0,1:T(8,128)}) %reduce-scatter.5.cloned.1.call-update) | async-done | bytes 2097168 | tf_op jit(solution)/shard_map/reduce_scatter | solution.py:38
  608.6 8.3 %multiply_add_fusion.1 = f32[2,256,1024]{2,1,0:T(8,128)} fusion(f32[2,256,1024]{2,1,0:T(8,128)} %param.13, f32[256,2,1024]{2,0,1:T(8,128)} %reduce-scatter.5.cloned.1.call-done, bf16[2,1024,1024]{2,1,0:T(8,128)(2,1)} %all-gather.5.cloned.1.call-done), kind=kOutput, calls=%fused_computation.5 | convolution fusion | flops 6443499520 | bytes 10485760 | tf_op jit(solution)/shard_map/mpk,pkc->mpc/dot_general | solution.py:45
  616.9 0.0 copy-done.1
Async XLA Ops:
  7.2 1.9 copy-start
  7.2 167.9 %all-gather.3.cloned.1.call-start = ((), (), s32[]{:S(2)}) async-start(), calls=%async_computation.2 | async-start | bytes 10485760 | tf_op jit(solution)/shard_map/all_gather | solution.py:18
  116.3 219.4 %all-reduce.3.cloned.1.call-start = ((), (), s32[]{:S(2)}) async-start(), calls=%async_computation.3 | async-start | bytes 8388608 | tf_op jit(solution)/shard_map/psum | solution.py:12
  180.6 200.5 %reduce-scatter.3.cloned.1.call-start = ((), (), s32[]{:S(2)}) async-start(), calls=%async_computation.4 | async-start | bytes 2359296 | tf_op jit(solution)/shard_map/reduce_scatter | solution.py:36
  340.8 122.4 %all-gather.5.cloned.1.call-start = ((), (), s32[]{:S(2)}) async-start(), calls=%async_computation.6 | async-start | bytes 5242880 | tf_op jit(solution)/shard_map/all_gather | solution.py:44
  341.4 267.2 %reduce-scatter.5.cloned.1.call-start = ((), (), s32[]{:S(2)}) async-start(), calls=%async_computation.5 | async-start | bytes 10485760 | tf_op jit(solution)/shard_map/reduce_scatter | solution.py:38
  357.6 23.5 %copy-start.2 = (f32[2,128,256]{2,1,0:T(8,128)S(1)}, f32[2,128,256]{2,1,0:T(8,128)}, u32[]{:S(2)}) copy-start(f32[2,128,256]{2,1,0:T(8,128)} %param.10) | copy-start | bytes 786436
  381.1 235.8 %copy-start.1 = (bf16[768,2048]{1,0:T(8,128)(2,1)S(1)}, bf16[768,2048]{1,0:T(8,128)(2,1)}, u32[]{:S(2)}) copy-start(bf16[768,2048]{1,0:T(8,128)(2,1)} %param.7) | copy-start | bytes 9437188
Sparse Core Ops, SparseCore 0:
  116.4 58.5 all-gather.2
  180.7 154.9 all-reduce.2
  340.9 40.0 reduce-scatter.2
  382.5 80.7 all-gather.4
  465.4 143.0 reduce-scatter.4
where the time goes:
time: 624 us; the launch traced here: 623 us
  waiting for transfers between devices  443 us (71%)
  blocking collectives  102 us (16%)
  matrix products  54.7 us (9%)
  between operations  13.8 us (2%)
  other arithmetic  7.33 us (1%)
    psum x1, waiting for transfers between devices, spread(): return lax.psum(jnp.where(mine, shard, jnp.zeros_like(shard)), axis)  155 us
    reduce_scatter x1, waiting for transfers between devices, shards(): lax.psum_scatter(jnp.einsum('pab,pbk->apk', left_root, grad_rows, preferr...  145 us
    psum x1, blocking collectives, shards(): summed = lax.psum(partial_grad, 'dp')  102 us
    all_gather x1, waiting for transfers between devices, shards(): lax.all_gather(right_root, 'grid', axis=1, tiled=True).astype(jnp.float32)  80.3 us
    all_gather x1, waiting for transfers between devices, shards(): lax.all_gather(summed.astype(jnp.bfloat16), 'tensor', axis=2, tiled=True)  58.7 us
    dot_general x1, matrix products, shards(): jnp.einsum('pak,pbk->pab', own_rows, grad_rows, preferred_element_type=jn...  20.4 us
    dot_general x1, matrix products, shards(): jnp.einsum('pab,pbk->apk', left_root, grad_rows, preferred_element_type=j...  15.9 us
  transfers between devices with their start and end apart: 5, of which 5 were waited for; matrix products, arithmetic and copies ran while one was open for 6% of the time, Pallas kernels for 0%

commit v1 on v0

--- a/solution.py
+++ b/solution.py
@@ -14,7 +14,8 @@
 
 def shards(tokens, cotangents, left_stat, right_stat, left_root, right_root, momentum):
     partial_grad = jnp.einsum("tr,pto->pro", tokens, cotangents, preferred_element_type=jnp.float32)
-    summed = lax.psum(partial_grad, "dp")
+    blocks = lax.all_gather(partial_grad, "dp")
+    summed = jnp.sum(blocks, axis=0)
     grad_rows = lax.all_gather(summed.astype(jnp.bfloat16), "tensor", axis=2, tiled=True)
     block_rows = left_stat.shape[1]
     grid_rows = left_stat.shape[2]

time: 624 us -> 641 us (1.027)
  waiting for transfers between devices: 443 us -> 552 us
  blocking collectives: 102 us -> 0 us
    all_gather x0 -> x1, waiting for transfers between devices: none -> 107 us  [shards(): blocks = lax.all_gather(partial_grad, 'dp')]
    psum x1 -> x0, blocking collectives: 102 us -> none  [shards(): summed = lax.psum(partial_grad, 'dp')]
  transfers between devices with their start and end apart: 5 -> 6, of which waited for: 5 -> 6; matrix products, arithmetic and copies ran while one was open for 6% -> 6% of each run, Pallas kernels for 0% -> 0%
where the time goes in v1:
time: 641 us
  waiting for transfers between devices  552 us (86%)
  matrix products  53.9 us (8%)
  between operations  14.2 us (2%)
  other arithmetic  13.3 us (2%)
  local copies, waits for them, and re-layouts  7.18 us (1%)
    psum x1, waiting for transfers between devices, spread(): return lax.psum(jnp.where(mine, shard, jnp.zeros_like(shard)), axis)  155 us
    reduce_scatter x1, waiting for transfers between devices, shards(): lax.psum_scatter(jnp.einsum('pab,pbk->apk', left_root, grad_rows, preferr...  145 us
    all_gather x1, waiting for transfers between devices, shards(): blocks = lax.all_gather(partial_grad, 'dp')  107 us
    all_gather x1, waiting for transfers between devices, shards(): lax.all_gather(right_root, 'grid', axis=1, tiled=True).astype(jnp.float32)  80.4 us
    all_gather x1, waiting for transfers between devices, shards(): lax.all_gather(summed.astype(jnp.bfloat16), 'tensor', axis=2, tiled=True)  59.5 us
    dot_general x1, matrix products, shards(): jnp.einsum('pak,pbk->pab', own_rows, grad_rows, preferred_element_type=jn...  19.3 us
    dot_general x1, matrix products, shards(): jnp.einsum('pab,pbk->apk', left_root, grad_rows, preferred_element_type=j...  15.8 us
  transfers between devices with their start and end apart: 6, of which 6 were waited for; matrix products, arithmetic and copies ran while one was open for 6% of the time, Pallas kernels for 0%

profile of v1, /device:TPU:0, one launch (start us, length us, event | category | flops | bytes accessed | tf_op | source)
XLA Modules:
  0.0 640.9 jit_solution(6445191900169032796)
XLA Ops:
  7.2 0.0 copy-start
  7.2 0.0 all-gather.9.cloned.1.call-start
  7.2 1.8 copy-done
  9.1 5.0 convolution_bitcast_fusion
  14.0 5.3 copy.13
  19.4 0.0 all-gather.9.cloned.1.call-update
  19.4 0.0 all-gather.5.cloned.1.call-start
  19.4 106.8 %all-gather.9.cloned.1.call-done = f32[4,2048,256]{2,1,0:T(8,128)} async-done(((f32[2,2048,256]{2,1,0:T(8,128)}), f32[4,2048,256]{2,1,0:T(8,128)}) %all-gather.9.cloned.1.call-update) | async-done | bytes 8388624 | tf_op jit(solution)/shard_map/all_gather | solution.py:17
  126.3 6.0 reduce_sum.9
  132.2 0.0 all-gather.5.cloned.1.call-update
  132.3 0.0 all-reduce.2.cloned.1.call-start
  132.4 59.5 %all-gather.5.cloned.1.call-done = bf16[2,2048,1024]{2,1,0:T(8,128)(2,1)} async-done(((bf16[2,2048,256]{2,1,0:T(8,128)(2,1)}), bf16[2,2048,1024]{2,1,0:T(8,128)(2,1)}) %all-gather.5.cloned.1.call-update) | async-done | bytes 8388624 | tf_op jit(solution)/shard_map/all_gather | solution.py:19
  191.8 5.5 dynamic-slice_select_fusion
  197.3 0.0 all-reduce.2.cloned.1.call-update
  197.3 0.0 reduce-scatter.3.cloned.1.call-start
  197.4 155.1 %all-reduce.2.cloned.1.call-done = bf16[2,1024,1024]{2,1,0:T(8,128)(2,1)} async-done(((bf16[2,1024,1024]{2,1,0:T(8,128)(2,1)}), bf16[2,1024,1024]{2,1,0:T(8,128)(2,1)}) %all-reduce.2.cloned.1.call-update) | async-done | bytes 4194320 | tf_op jit(solution)/shard_map/psum | solution.py:12
  352.5 5.5 fusion.1
  358.0 0.0 reduce-scatter.3.cloned.1.call-update
  358.0 0.0 all-gather.7.cloned.1.call-start
  358.1 0.5 all-gather.7.cloned.1.call-update
  358.6 0.2 reduce-scatter.5.cloned.1.call-start
  358.8 15.8 %convolution_bitcast_fusion.1 = f32[1024,2,1024]{2,0,1:T(8,128)} fusion(bf16[2,1024,2048]{2,1,0:T(8,128)(2,1)} %param.11, bf16[2,2048,1024]{2,1,0:T(8,128)(2,1)} %all-gather.5.cloned.1.call-done), kind=kOutput, calls=%fused_computation.3 | convolution fusion | flops 8589934592 | bytes 25165824 | tf_op jit(solution)/shard_map/pab,pbk->apk/dot_general | solution.py:40
  374.6 0.0 reduce-scatter.5.cloned.1.call-update
  374.7 0.0 copy-start.2
  374.7 19.3 %multiply_add_fusion = f32[2,1024,2048]{2,1,0:T(8,128)} fusion(f32[2,1024,2048]{2,1,0:T(8,128)} %param.9, bf16[2,1024,1024]{2,1,0:T(8,128)(2,1)} %all-reduce.2.cloned.1.call-done, bf16[2,2048,1024]{2,1,0:T(8,128)(2,1)} %all-gather.5.cloned.1.call-done), kind=kOutput, calls=%fused_computation | convolution fusion | flops 8602517504 | bytes 46137344 | tf_op jit(solution)/shard_map/pak,pbk->pab/dot_general | solution.py:28
  394.0 4.2 reduce-scatter.3.cloned.1.call-done
  398.3 0.0 copy-done.2
  398.3 0.0 copy-start.1
  398.3 1.8 multiply_add_fusion.2
  400.1 80.4 %all-gather.7.cloned.1.call-done = bf16[2,1024,1024]{2,1,0:T(8,128)(2,1)} async-done(((bf16[2,256,1024]{2,1,0:T(8,128)(2,1)}), bf16[2,1024,1024]{2,1,0:T(8,128)(2,1)}) %all-gather.7.cloned.1.call-update) | async-done | bytes 4194320 | tf_op jit(solution)/shard_map/all_gather | solution.py:45
  480.5 145.3 %reduce-scatter.5.cloned.1.call-done = f32[256,2,1024]{2,0,1:T(8,128)} async-done(((f32[1024,2,1024]{2,0,1:T(8,128)}), f32[256,2,1024]{2,0,1:T(8,128)}) %reduce-scatter.5.cloned.1.call-update) | async-done | bytes 2097168 | tf_op jit(solution)/shard_map/reduce_scatter | solution.py:39
  625.8 8.3 %multiply_add_fusion.1 = f32[2,256,1024]{2,1,0:T(8,128)} fusion(f32[2,256,1024]{2,1,0:T(8,128)} %param.13, f32[256,2,1024]{2,0,1:T(8,128)} %reduce-scatter.5.cloned.1.call-done, bf16[2,1024,1024]{2,1,0:T(8,128)(2,1)} %all-gather.7.cloned.1.call-done), kind=kOutput, calls=%fused_computation.5 | convolution fusion | flops 6443499520 | bytes 10485760 | tf_op jit(solution)/shard_map/mpk,pkc->mpc/dot_general | solution.py:46
  634.1 0.0 copy-done.1
Async XLA Ops:
  7.2 1.9 copy-start
  7.2 119.1 %all-gather.9.cloned.1.call-start = ((), (), s32[]{:S(2)}) async-start(), calls=%async_computation.7 | async-start | bytes 12582912 | tf_op jit(solution)/shard_map/all_gather | solution.py:17
  19.4 172.4 %all-gather.5.cloned.1.call-start = ((), (), s32[]{:S(2)}) async-start(), calls=%async_computation.2 | async-start | bytes 10485760 | tf_op jit(solution)/shard_map/all_gather | solution.py:19
  132.3 220.2 %all-reduce.2.cloned.1.call-start = ((), (), s32[]{:S(2)}) async-start(), calls=%async_computation.3 | async-start | bytes 8388608 | tf_op jit(solution)/shard_map/psum | solution.py:12
  197.3 200.9 %reduce-scatter.3.cloned.1.call-start = ((), (), s32[]{:S(2)}) async-start(), calls=%async_computation.4 | async-start | bytes 2359296 | tf_op jit(solution)/shard_map/reduce_scatter | solution.py:37
  358.0 122.5 %all-gather.7.cloned.1.call-start = ((), (), s32[]{:S(2)}) async-start(), calls=%async_computation.6 | async-start | bytes 5242880 | tf_op jit(solution)/shard_map/all_gather | solution.py:45
  358.6 267.2 %reduce-scatter.5.cloned.1.call-start = ((), (), s32[]{:S(2)}) async-start(), calls=%async_computation.5 | async-start | bytes 10485760 | tf_op jit(solution)/shard_map/reduce_scatter | solution.py:39
  374.7 23.6 %copy-start.2 = (f32[2,128,256]{2,1,0:T(8,128)S(1)}, f32[2,128,256]{2,1,0:T(8,128)}, u32[]{:S(2)}) copy-start(f32[2,128,256]{2,1,0:T(8,128)} %param.10) | copy-start | bytes 786436
  398.3 235.8 %copy-start.1 = (bf16[768,2048]{1,0:T(8,128)(2,1)S(1)}, bf16[768,2048]{1,0:T(8,128)(2,1)}, u32[]{:S(2)}) copy-start(bf16[768,2048]{1,0:T(8,128)(2,1)} %param.7) | copy-start | bytes 9437188
Sparse Core Ops, SparseCore 0:
  19.5 106.6 all-gather.8
  132.4 59.3 all-gather.4
  197.4 154.9 all-reduce.1
  358.1 40.0 reduce-scatter.2
  399.7 80.7 all-gather.6
  482.7 143.0 reduce-scatter.4
